TPU v7x, 32 devices: a whole 2x2x4 slice. The times are simulated.
32 devices in a mesh: az: 4 (over y, x), rad: 8 (over z, core).
Axes of the slice: x: 2, y: 2, z: 4, core: 2. Of those that a mesh axis runs over, the one named last changes fastest.
Arguments:
- fields: float32 [5, 96, 32, 512], P(None, 'rad', None, 'az'), may hold values from -6 to 6
- shift: int32 [96], replicated, may hold values from 0 to 511
- fraction: float32 [96], replicated, may hold values from -0.5 to 0.5
- radial_rate: float32 [96, 32], replicated, may hold values from -0.4 to 0.4
Outputs:
- updated: float32 [5, 96, 32, 512], P(None, 'rad', None, 'az')
All inputs are finite; a program needn't handle non-finite values.
Results may differ from a plain program's by a relative error of at most 0.0003.
Values sent between devices are 32-bit elements; how exact they have to be, the bound alone decides.
No kernel may reach another device: no remote copies, remote signals or barrier semaphores. Data moves between devices by JAX's collectives and lax.ppermute only.
A program may use at most 64 MiB of HBM per device.

v0:
```python
import functools

import jax
import jax.numpy as jnp
from jax import lax
from jax.experimental import pallas as pl
from jax.experimental.pallas import tpu as pltpu
from jax.sharding import PartitionSpec as P


def pick(table, position):
    chosen = jnp.int32(table[0])
    for place, entry in enumerate(table[1:], 1):
        chosen = jnp.where(position == place, jnp.int32(entry), chosen)
    return chosen


def limited(left, right):
    bound = jnp.where(
        left * right > 0.0, 2.0 * jnp.minimum(jnp.abs(left), jnp.abs(right)), 0.0
    )
    return jnp.maximum(jnp.minimum(0.5 * (left + right), bound), -bound)


def plan(rows, group):
    edges = [0, 1, rows - 2, rows - 1]
    inner = [row for row in range(rows) if row not in edges]
    first = edges + inner[: group - len(edges)]
    rest = inner[group - len(edges):]
    each = len(rest) // group
    starts = [rest[device * each] for device in range(group)] if each else []
    return first, starts, each


def kept(array):
    return pltpu.with_memory_space_constraint(array, pltpu.VMEM)


def pack_kernel(table, rows, fields, turned, *refs):
    group = len(table)
    results, rates, sems = (refs[:group], refs[group:-1], refs[-1])
    here = lax.axis_index("az")
    copies = []
    for place, result in enumerate(results):
        rotated = [table[(device + place) % group] for device in range(group)]
        source = fields.at[:, pl.ds(pick(rotated, here), result.shape[1])]
        copies.append(pltpu.make_async_copy(source, result, sems.at[place]))
    for copy in copies:
        copy.start()
    if rates:
        spread_rates(turned, rates[0], lax.axis_index("rad") * rows - 1)
    for copy in copies:
        copy.wait()


def spread_rates(turned, result, below):
    columns = turned[...]
    place = lax.broadcasted_iota(jnp.int32, columns.shape, 1)
    inside = jnp.where(place < columns.shape[1] - 1, columns, 0.0)
    for row in range(result.shape[0]):
        column = jnp.sum(jnp.where(place == below + row, inside, 0.0), axis=1, keepdims=True)
        result[row] = jnp.broadcast_to(column, result.shape[1:])


def pack(fields, radial_rate, table, count, with_rates):
    group, rows = (len(table), fields.shape[1])
    shape = (fields.shape[0], count) + fields.shape[2:]
    kinds = [pltpu.VMEM(shape, fields.dtype)] * group
    kinds += [pltpu.VMEM((rows + 1,) + fields.shape[2:], jnp.float32)] * with_rates
    vmem = pl.BlockSpec(memory_space=pltpu.VMEM)
    return pl.pallas_call(
        functools.partial(pack_kernel, table, rows),
        out_shape=kinds,
        in_specs=[pl.BlockSpec(memory_space=pl.ANY), vmem if with_rates else pl.BlockSpec(memory_space=pl.ANY)],
        out_specs=[vmem] * len(kinds),
        scratch_shapes=[pltpu.SemaphoreType.DMA((group,))],
        name="pack",
    )(fields, radial_rate.T)


def azimuthal_kernel(starts, rows, shift, fraction, *refs):
    group = len(refs) // 2
    parts, results = (refs[:group], refs[group:])
    fields, count, polar, width = parts[0].shape
    cycle = group * width
    first = lax.axis_index("rad") * rows + pick(starts, lax.axis_index("az"))
    for step in range(count):
        move = shift[first + step]
        courant = fraction[first + step]
        ahead = courant > 0.0
        weight = jnp.where(ahead, 0.5 * (1.0 - courant), -0.5 * (1.0 + courant))
        cells = jnp.concatenate(
            [
                parts[(group - place) % group][:, step].reshape(fields * polar, width)
                for place in range(group)
            ],
            axis=1,
        )
        right = pltpu.roll(cells, cycle - 1, 1) - cells
        face = cells + weight * limited(pltpu.roll(right, 1, 1), right)
        change = face - pltpu.roll(face, 1, 1)
        change = jnp.where(ahead, change, pltpu.roll(change, cycle - 1, 1))
        final = pltpu.roll(cells - courant * change, move, 1)
        for place in range(group):
            results[place][:, step] = final[:, place * width:(place + 1) * width].reshape(
                fields, polar, width
            )


def azimuthal(parts, starts, rows, shift, fraction):
    vmem = pl.BlockSpec(memory_space=pltpu.VMEM)
    smem = pl.BlockSpec(memory_space=pltpu.SMEM)
    return pl.pallas_call(
        functools.partial(azimuthal_kernel, starts, rows),
        out_shape=[pltpu.VMEM(part.shape, part.dtype) for part in parts],
        in_specs=[smem, smem] + [vmem] * len(parts),
        out_specs=[vmem] * len(parts),
        name="azimuthal",
    )(shift, fraction, *map(kept, parts))


def radial_kernel(places, rows, rates, *refs):
    count = len(places)
    parts, result, cells, done, sems = (refs[:count],) + refs[count:]
    here = lax.axis_index("az")
    starts = [pick(place, here) for place in places]
    copies = []
    for field in range(parts[0].shape[0]):
        for part, start in zip(parts, starts):
            for step in range(part.shape[1]):
                cells[field, start + step] = part[field, step]
        flow(cells.at[field], rates, done.at[field], rows)
        copies.append(pltpu.make_async_copy(done.at[field], result.at[field], sems.at[field]))
        copies[-1].start()
    for copy in copies:
        copy.wait()


def flow(cells, rates, result, rows):
    before, middle = (cells[0], cells[1])
    left = middle - before
    slope_before = cell_before = flux_before = None
    for row in range(rows + 2):
        after = cells[row + 2]
        right = after - middle
        slope = limited(left, right)
        if row:
            courant = rates[row - 1]
            forward = cell_before + 0.5 * (1.0 - courant) * slope_before
            backward = middle - 0.5 * (1.0 + courant) * slope
            flux = courant * jnp.where(courant > 0.0, forward, backward)
            if row > 1:
                result[row - 2] = cell_before - (flux - flux_before)
            flux_before = flux
        slope_before, cell_before, middle, left = (slope, middle, after, right)


def radial(parts, places, rates, rows):
    fields, _, polar, width = parts[0].shape
    vmem = pl.BlockSpec(memory_space=pltpu.VMEM)
    shape = (fields, rows, polar, width)
    return pl.pallas_call(
        functools.partial(radial_kernel, places, rows),
        out_shape=jax.ShapeDtypeStruct(shape, jnp.float32),
        in_specs=[vmem] * (1 + len(parts)),
        out_specs=pl.BlockSpec(memory_space=pl.ANY),
        scratch_shapes=[
            pltpu.VMEM((fields, rows + 4, polar, width), jnp.float32),
            pltpu.VMEM(shape, jnp.float32),
            pltpu.SemaphoreType.DMA((fields,)),
        ],
        name="radial",
    )(kept(rates), *map(kept, parts))


def edges_kernel(*refs):
    parts, results = (refs[:-2], refs[-2:])
    group, here = (len(parts), lax.axis_index("az"))
    for edge in range(4):
        source = lax.rem(here - edge + group, group)
        for field in range(parts[0].shape[0]):
            chosen = parts[0][field, 0]
            for k in range(1, group):
                chosen = jnp.where(source == k, parts[k][field, 0], chosen)
            results[edge // 2][field, edge % 2] = chosen


def edges(parts):
    fields, _, polar, width = parts[0].shape
    vmem = pl.BlockSpec(memory_space=pltpu.VMEM)
    return pl.pallas_call(
        edges_kernel,
        out_shape=[pltpu.VMEM((fields, 2, polar, width), jnp.float32)] * 2,
        in_specs=[vmem] * len(parts),
        out_specs=[vmem] * 2,
        name="edges",
    )(*map(kept, parts))


def exchange(parts, group):
    moved = [parts[0]]
    for k in range(1, group):
        moved.append(lax.ppermute(parts[k], "az", [(i, (i + k) % group) for i in range(group)]))
    return moved


def substep(fields, shift, fraction, radial_rate):
    rows = fields.shape[1]
    group, blocks = (lax.axis_size("az"), lax.axis_size("rad"))
    first, starts, each = plan(rows, group)
    sets = [(first, 1)] + ([(starts, each)] if each else [])
    cycles = []
    for turn, (table, count) in enumerate(sets):
        last = turn == len(sets) - 1
        packed = pack(fields, radial_rate, table, count, last)
        cycles.append(exchange(packed[:group], group))
    rates = packed[group]
    parts, places = ([], [])
    for (table, count), cycle in zip(sets, cycles):
        updated = azimuthal(cycle, table, rows, shift, fraction)
        parts += exchange(updated, group)
        for k in range(group):
            places.append([2 + table[(i - k) % group] for i in range(group)])
    low, high = edges(parts[:group])
    up = [(b, b + 1) for b in range(blocks - 1)]
    down = [(b, a) for a, b in up]
    parts.append(lax.ppermute(high, "rad", up))
    parts.append(lax.ppermute(low, "rad", down))
    places += [[0] * group, [rows + 2] * group]
    return radial(parts, places, rates, rows)


def solution(mesh):
    placed = (P(None, "rad", None, "az"), P(), P(), P())
    return jax.shard_map(
        substep, mesh=mesh, in_specs=placed, out_specs=P(None, "rad", None, "az"), check_vma=False
    )
```

profile of v0, /device:TPU:18, one launch (start us, length us, event | category | flops | bytes accessed | tf_op | source)
XLA Modules:
  0.0 45.2 jit_solution(7527158672772881383)
XLA Ops:
  0.0 1.0 %pack.3 = (f32[5,1,32,128]{3,2,1,0:T(8,128)S(1)}, f32[5,1,32,128]{3,2,1,0:T(8,128)S(1)}, f32[5,1,32,128]{3,2,1,0:T(8,128)S(1)}, f32[5,1,32,128]{3,2,1,0:T(8,128)S(1)}) custom-call(f32[5,12,32,128]{3,2,1,0:T(8,128)} %fields.3, f32[32,96]{1,0:T(8,128)} %bitcast.1), custom_call_target="tpu_custom_call" | custom-call | tf_op jit(solution)/shard_map/pack/pallas_call | solution.py:71
  1.0 1.5 %collective-permute-start = (f32[5,1,32,128]{3,2,1,0:T(8,128)S(1)}, f32[5,1,32,128]{3,2,1,0:T(8,128)S(1)}, u32[]{:S(2)}, u32[]{:S(2)}) collective-permute-start(f32[5,1,32,128]{3,2,1,0:T(8,128)S(1)} %get-tuple-element.26), channel_id=1, source_target_pairs={{0,8},{8,16},{16,24},{24,0},{1,9},{9,17},{17,25},{25,1},{2,10},{10... | collective-permute-start | bytes 245768 | tf_op jit(solution)/shard_map/ppermute | solution.py:203
  2.6 0.5 %collective-permute-start.1 = (f32[5,1,32,128]{3,2,1,0:T(8,128)S(1)}, f32[5,1,32,128]{3,2,1,0:T(8,128)S(1)}, u32[]{:S(2)}, u32[]{:S(2)}) collective-permute-start(f32[5,1,32,128]{3,2,1,0:T(8,128)S(1)} %get-tuple-element.27), channel_id=1, source_target_pairs={{0,16},{8,24},{16,0},{24,8},{1,17},{9,25},{17,1},{25,9},{2,18},{10... | collective-permute-start | bytes 245768 | tf_op jit(solution)/shard_map/ppermute | solution.py:203
  3.1 1.5 %collective-permute-start.2 = (f32[5,1,32,128]{3,2,1,0:T(8,128)S(1)}, f32[5,1,32,128]{3,2,1,0:T(8,128)S(1)}, u32[]{:S(2)}, u32[]{:S(2)}) collective-permute-start(f32[5,1,32,128]{3,2,1,0:T(8,128)S(1)} %get-tuple-element.28), channel_id=1, source_target_pairs={{0,24},{8,0},{16,8},{24,16},{1,25},{9,1},{17,9},{25,17},{2,26},{10... | collective-permute-start | bytes 245768 | tf_op jit(solution)/shard_map/ppermute | solution.py:203
  4.6 0.9 %collective-permute-done.refs_1_ = f32[5,1,32,128]{3,2,1,0:T(8,128)S(1)} collective-permute-done((f32[5,1,32,128]{3,2,1,0:T(8,128)S(1)}, f32[5,1,32,128]{3,2,1,0:T(8,128)S(1)}, u32[]{:S(2)}, u32[]{:S(2)}) %collective-permute-start) | collective-permute-done | bytes 81952 | tf_op jit(solution)/shard_map/ppermute | solution.py:203
  5.5 3.1 %collective-permute-done.1.refs_2_ = f32[5,1,32,128]{3,2,1,0:T(8,128)S(1)} collective-permute-done((f32[5,1,32,128]{3,2,1,0:T(8,128)S(1)}, f32[5,1,32,128]{3,2,1,0:T(8,128)S(1)}, u32[]{:S(2)}, u32[]{:S(2)}) %collective-permute-start.1) | collective-permute-done | bytes 81952 | tf_op jit(solution)/shard_map/ppermute | solution.py:203
  8.6 1.3 %azimuthal.2 = (f32[5,1,32,128]{3,2,1,0:T(8,128)S(1)}, f32[5,1,32,128]{3,2,1,0:T(8,128)S(1)}, f32[5,1,32,128]{3,2,1,0:T(8,128)S(1)}, f32[5,1,32,128]{3,2,1,0:T(8,128)S(1)}) custom-call(s32[96]{0:T(128)} %shift.3, f32[96]{0:T(128)} %fraction.3, f32[5,1,32,128]{3,2,1,0:T(8,128)S(1)} %get-tuple-element.25.refs_0_, ...), custom_call_target="tpu_custom_call" | custom-call | tf_op jit(solution)/shard_map/azimuthal/pallas_call | solution.py:113
  10.0 0.8 %collective-permute-start.3 = (f32[5,1,32,128]{3,2,1,0:T(8,128)S(1)}, f32[5,1,32,128]{3,2,1,0:T(8,128)S(1)}, u32[]{:S(2)}, u32[]{:S(2)}) collective-permute-start(f32[5,1,32,128]{3,2,1,0:T(8,128)S(1)} %get-tuple-element.30), channel_id=1, source_target_pairs={{0,8},{8,16},{16,24},{24,0},{1,9},{9,17},{17,25},{25,1},{2,10},{10... | collective-permute-start | bytes 245768 | tf_op jit(solution)/shard_map/ppermute | solution.py:203
  10.8 1.9 %pack.2 = (f32[5,2,32,128]{3,2,1,0:T(8,128)S(1)}, f32[5,2,32,128]{3,2,1,0:T(8,128)S(1)}, f32[5,2,32,128]{3,2,1,0:T(8,128)S(1)}, f32[5,2,32,128]{3,2,1,0:T(8,128)S(1)}, f32[13,32,128]{2,1,0:T(8,128)S(1)}) custom-call(f32[5,12,32,128]{3,2,1,0:T(8,128)} %fields.3, f32[32,96]{1,0:T(8,128)} %bitcast.2), custom_call_target="tpu_custom_call" | custom-call | tf_op jit(solution)/shard_map/pack/pallas_call | solution.py:71
  12.7 2.0 %collective-permute-start.6 = (f32[5,2,32,128]{3,2,1,0:T(8,128)S(1)}, f32[5,2,32,128]{3,2,1,0:T(8,128)S(1)}, u32[]{:S(2)}, u32[]{:S(2)}) collective-permute-start(f32[5,2,32,128]{3,2,1,0:T(8,128)S(1)} %get-tuple-element.34), channel_id=1, source_target_pairs={{0,8},{8,16},{16,24},{24,0},{1,9},{9,17},{17,25},{25,1},{2,10},{10... | collective-permute-start | bytes 491528 | tf_op jit(solution)/shard_map/ppermute | solution.py:203
  14.8 0.7 %collective-permute-start.7 = (f32[5,2,32,128]{3,2,1,0:T(8,128)S(1)}, f32[5,2,32,128]{3,2,1,0:T(8,128)S(1)}, u32[]{:S(2)}, u32[]{:S(2)}) collective-permute-start(f32[5,2,32,128]{3,2,1,0:T(8,128)S(1)} %get-tuple-element.35), channel_id=1, source_target_pairs={{0,16},{8,24},{16,0},{24,8},{1,17},{9,25},{17,1},{25,9},{2,18},{10... | collective-permute-start | bytes 491528 | tf_op jit(solution)/shard_map/ppermute | solution.py:203
  15.5 0.4 collective-permute-start.8
  15.9 0.9 %collective-permute-start.4 = (f32[5,1,32,128]{3,2,1,0:T(8,128)S(1)}, f32[5,1,32,128]{3,2,1,0:T(8,128)S(1)}, u32[]{:S(2)}, u32[]{:S(2)}) collective-permute-start(f32[5,1,32,128]{3,2,1,0:T(8,128)S(1)} %get-tuple-element.31), channel_id=1, source_target_pairs={{0,16},{8,24},{16,0},{24,8},{1,17},{9,25},{17,1},{25,9},{2,18},{10... | collective-permute-start | bytes 245768 | tf_op jit(solution)/shard_map/ppermute | solution.py:203
  16.9 2.1 %collective-permute-start.5 = (f32[5,1,32,128]{3,2,1,0:T(8,128)S(1)}, f32[5,1,32,128]{3,2,1,0:T(8,128)S(1)}, u32[]{:S(2)}, u32[]{:S(2)}) collective-permute-start(f32[5,1,32,128]{3,2,1,0:T(8,128)S(1)} %get-tuple-element.32), channel_id=1, source_target_pairs={{0,24},{8,0},{16,8},{24,16},{1,25},{9,1},{17,9},{25,17},{2,26},{10... | collective-permute-start | bytes 245768 | tf_op jit(solution)/shard_map/ppermute | solution.py:203
  19.0 6.6 %collective-permute-done.4.refs_2_ = f32[5,1,32,128]{3,2,1,0:T(8,128)S(1)} collective-permute-done((f32[5,1,32,128]{3,2,1,0:T(8,128)S(1)}, f32[5,1,32,128]{3,2,1,0:T(8,128)S(1)}, u32[]{:S(2)}, u32[]{:S(2)}) %collective-permute-start.4) | collective-permute-done | bytes 81952 | tf_op jit(solution)/shard_map/ppermute | solution.py:203
  25.7 1.9 %collective-permute-start.12 = (f32[5,2,32,128]{3,2,1,0:T(8,128)S(1)}, f32[5,2,32,128]{3,2,1,0:T(8,128)S(1)}, u32[]{:S(2)}, u32[]{:S(2)}) collective-permute-start(f32[5,2,32,128]{3,2,1,0:T(8,128)S(1)} %get-tuple-element.41), channel_id=1, source_target_pairs={{0,1},{1,2},{2,3},{3,4},{4,5},{5,6},{6,7},{8,9},{9,10},{10,11},{11... | collective-permute-start | bytes 491528 | tf_op jit(solution)/shard_map/ppermute | solution.py:227
  27.6 3.6 %collective-permute-start.13 = (f32[5,2,32,128]{3,2,1,0:T(8,128)S(1)}, f32[5,2,32,128]{3,2,1,0:T(8,128)S(1)}, u32[]{:S(2)}, u32[]{:S(2)}) collective-permute-start(f32[5,2,32,128]{3,2,1,0:T(8,128)S(1)} %get-tuple-element.42), channel_id=1, source_target_pairs={{1,0},{2,1},{3,2},{4,3},{5,4},{6,5},{7,6},{9,8},{10,9},{11,10},{12... | collective-permute-start | bytes 491528 | tf_op jit(solution)/shard_map/ppermute | solution.py:228
  31.3 1.9 %azimuthal.3 = (f32[5,2,32,128]{3,2,1,0:T(8,128)S(1)}, f32[5,2,32,128]{3,2,1,0:T(8,128)S(1)}, f32[5,2,32,128]{3,2,1,0:T(8,128)S(1)}, f32[5,2,32,128]{3,2,1,0:T(8,128)S(1)}) custom-call(s32[96]{0:T(128)} %shift.3, f32[96]{0:T(128)} %fraction.3, f32[5,2,32,128]{3,2,1,0:T(8,128)S(1)} %get-tuple-element.33.refs_0_, ...), custom_call_target="tpu_custom_call" | custom-call | tf_op jit(solution)/shard_map/azimuthal/pallas_call | solution.py:113
  33.2 0.1 collective-permute-start.9
  33.3 1.3 %collective-permute-start.10 = (f32[5,2,32,128]{3,2,1,0:T(8,128)S(1)}, f32[5,2,32,128]{3,2,1,0:T(8,128)S(1)}, u32[]{:S(2)}, u32[]{:S(2)}) collective-permute-start(f32[5,2,32,128]{3,2,1,0:T(8,128)S(1)} %get-tuple-element.39), channel_id=1, source_target_pairs={{0,16},{8,24},{16,0},{24,8},{1,17},{9,25},{17,1},{25,9},{2,18},{10... | collective-permute-start | bytes 491528 | tf_op jit(solution)/shard_map/ppermute | solution.py:203
  34.6 1.9 %collective-permute-start.11 = (f32[5,2,32,128]{3,2,1,0:T(8,128)S(1)}, f32[5,2,32,128]{3,2,1,0:T(8,128)S(1)}, u32[]{:S(2)}, u32[]{:S(2)}) collective-permute-start(f32[5,2,32,128]{3,2,1,0:T(8,128)S(1)} %get-tuple-element.40), channel_id=1, source_target_pairs={{0,24},{8,0},{16,8},{24,16},{1,25},{9,1},{17,9},{25,17},{2,26},{10... | collective-permute-start | bytes 491528 | tf_op jit(solution)/shard_map/ppermute | solution.py:203
  36.5 3.8 %collective-permute-done.9.refs_5_ = f32[5,2,32,128]{3,2,1,0:T(8,128)S(1)} collective-permute-done((f32[5,2,32,128]{3,2,1,0:T(8,128)S(1)}, f32[5,2,32,128]{3,2,1,0:T(8,128)S(1)}, u32[]{:S(2)}, u32[]{:S(2)}) %collective-permute-start.9) | collective-permute-done | bytes 163872 | tf_op jit(solution)/shard_map/ppermute | solution.py:203
  40.3 3.2 %collective-permute-done.11.refs_7_ = f32[5,2,32,128]{3,2,1,0:T(8,128)S(1)} collective-permute-done((f32[5,2,32,128]{3,2,1,0:T(8,128)S(1)}, f32[5,2,32,128]{3,2,1,0:T(8,128)S(1)}, u32[]{:S(2)}, u32[]{:S(2)}) %collective-permute-start.11) | collective-permute-done | bytes 163872 | tf_op jit(solution)/shard_map/ppermute | solution.py:203
  43.5 1.6 %radial.1 = f32[5,12,32,128]{3,2,1,0:T(8,128)} custom-call(f32[13,32,128]{2,1,0:T(8,128)S(1)} %get-tuple-element.24.rates, f32[5,1,32,128]{3,2,1,0:T(8,128)S(1)} %get-tuple-element.29.refs_0_, f32[5,1,32,128]{3,2,1,0:T(8,128)S(1)} %collective-permute-done.3.refs_1_, f32[5,1,32,128]{3,2,1,0:T(8,128)S(1)} %collective-permute-done.4.refs_2_, ...), custom_call_target="tpu_custom_call" | custom-call | tf_op jit(solution)/shard_map/radial/pallas_call | solution.py:162
  (10 shorter events, 0.1 us)
Async XLA Ops:
  1.0 4.5 %collective-permute-start = (f32[5,1,32,128]{3,2,1,0:T(8,128)S(1)}, f32[5,1,32,128]{3,2,1,0:T(8,128)S(1)}, u32[]{:S(2)}, u32[]{:S(2)}) collective-permute-start(f32[5,1,32,128]{3,2,1,0:T(8,128)S(1)} %get-tuple-element.26), channel_id=1, source_target_pairs={{0,8},{8,16},{16,24},{24,0},{1,9},{9,17},{17,25},{25,1},{2,10},{10... | collective-permute-start | bytes 245768 | tf_op jit(solution)/shard_map/ppermute | solution.py:203
  2.6 6.1 %collective-permute-start.1 = (f32[5,1,32,128]{3,2,1,0:T(8,128)S(1)}, f32[5,1,32,128]{3,2,1,0:T(8,128)S(1)}, u32[]{:S(2)}, u32[]{:S(2)}) collective-permute-start(f32[5,1,32,128]{3,2,1,0:T(8,128)S(1)} %get-tuple-element.27), channel_id=1, source_target_pairs={{0,16},{8,24},{16,0},{24,8},{1,17},{9,25},{17,1},{25,9},{2,18},{10... | collective-permute-start | bytes 245768 | tf_op jit(solution)/shard_map/ppermute | solution.py:203
  3.1 5.5 %collective-permute-start.2 = (f32[5,1,32,128]{3,2,1,0:T(8,128)S(1)}, f32[5,1,32,128]{3,2,1,0:T(8,128)S(1)}, u32[]{:S(2)}, u32[]{:S(2)}) collective-permute-start(f32[5,1,32,128]{3,2,1,0:T(8,128)S(1)} %get-tuple-element.28), channel_id=1, source_target_pairs={{0,24},{8,0},{16,8},{24,16},{1,25},{9,1},{17,9},{25,17},{2,26},{10... | collective-permute-start | bytes 245768 | tf_op jit(solution)/shard_map/ppermute | solution.py:203
  10.0 6.9 %collective-permute-start.3 = (f32[5,1,32,128]{3,2,1,0:T(8,128)S(1)}, f32[5,1,32,128]{3,2,1,0:T(8,128)S(1)}, u32[]{:S(2)}, u32[]{:S(2)}) collective-permute-start(f32[5,1,32,128]{3,2,1,0:T(8,128)S(1)} %get-tuple-element.30), channel_id=1, source_target_pairs={{0,8},{8,16},{16,24},{24,0},{1,9},{9,17},{17,25},{25,1},{2,10},{10... | collective-permute-start | bytes 245768 | tf_op jit(solution)/shard_map/ppermute | solution.py:203
  12.7 18.5 %collective-permute-start.6 = (f32[5,2,32,128]{3,2,1,0:T(8,128)S(1)}, f32[5,2,32,128]{3,2,1,0:T(8,128)S(1)}, u32[]{:S(2)}, u32[]{:S(2)}) collective-permute-start(f32[5,2,32,128]{3,2,1,0:T(8,128)S(1)} %get-tuple-element.34), channel_id=1, source_target_pairs={{0,8},{8,16},{16,24},{24,0},{1,9},{9,17},{17,25},{25,1},{2,10},{10... | collective-permute-start | bytes 491528 | tf_op jit(solution)/shard_map/ppermute | solution.py:203
  14.8 16.5 %collective-permute-start.7 = (f32[5,2,32,128]{3,2,1,0:T(8,128)S(1)}, f32[5,2,32,128]{3,2,1,0:T(8,128)S(1)}, u32[]{:S(2)}, u32[]{:S(2)}) collective-permute-start(f32[5,2,32,128]{3,2,1,0:T(8,128)S(1)} %get-tuple-element.35), channel_id=1, source_target_pairs={{0,16},{8,24},{16,0},{24,8},{1,17},{9,25},{17,1},{25,9},{2,18},{10... | collective-permute-start | bytes 491528 | tf_op jit(solution)/shard_map/ppermute | solution.py:203
  15.5 15.8 %collective-permute-start.8 = (f32[5,2,32,128]{3,2,1,0:T(8,128)S(1)}, f32[5,2,32,128]{3,2,1,0:T(8,128)S(1)}, u32[]{:S(2)}, u32[]{:S(2)}) collective-permute-start(f32[5,2,32,128]{3,2,1,0:T(8,128)S(1)} %get-tuple-element.36), channel_id=1, source_target_pairs={{0,24},{8,0},{16,8},{24,16},{1,25},{9,1},{17,9},{25,17},{2,26},{10... | collective-permute-start | bytes 491528 | tf_op jit(solution)/shard_map/ppermute | solution.py:203
  15.9 9.7 %collective-permute-start.4 = (f32[5,1,32,128]{3,2,1,0:T(8,128)S(1)}, f32[5,1,32,128]{3,2,1,0:T(8,128)S(1)}, u32[]{:S(2)}, u32[]{:S(2)}) collective-permute-start(f32[5,1,32,128]{3,2,1,0:T(8,128)S(1)} %get-tuple-element.31), channel_id=1, source_target_pairs={{0,16},{8,24},{16,0},{24,8},{1,17},{9,25},{17,1},{25,9},{2,18},{10... | collective-permute-start | bytes 245768 | tf_op jit(solution)/shard_map/ppermute | solution.py:203
  16.9 8.7 %collective-permute-start.5 = (f32[5,1,32,128]{3,2,1,0:T(8,128)S(1)}, f32[5,1,32,128]{3,2,1,0:T(8,128)S(1)}, u32[]{:S(2)}, u32[]{:S(2)}) collective-permute-start(f32[5,1,32,128]{3,2,1,0:T(8,128)S(1)} %get-tuple-element.32), channel_id=1, source_target_pairs={{0,24},{8,0},{16,8},{24,16},{1,25},{9,1},{17,9},{25,17},{2,26},{10... | collective-permute-start | bytes 245768 | tf_op jit(solution)/shard_map/ppermute | solution.py:203
  25.7 10.9 %collective-permute-start.12 = (f32[5,2,32,128]{3,2,1,0:T(8,128)S(1)}, f32[5,2,32,128]{3,2,1,0:T(8,128)S(1)}, u32[]{:S(2)}, u32[]{:S(2)}) collective-permute-start(f32[5,2,32,128]{3,2,1,0:T(8,128)S(1)} %get-tuple-element.41), channel_id=1, source_target_pairs={{0,1},{1,2},{2,3},{3,4},{4,5},{5,6},{6,7},{8,9},{9,10},{10,11},{11... | collective-permute-start | bytes 491528 | tf_op jit(solution)/shard_map/ppermute | solution.py:227
  27.6 8.9 %collective-permute-start.13 = (f32[5,2,32,128]{3,2,1,0:T(8,128)S(1)}, f32[5,2,32,128]{3,2,1,0:T(8,128)S(1)}, u32[]{:S(2)}, u32[]{:S(2)}) collective-permute-start(f32[5,2,32,128]{3,2,1,0:T(8,128)S(1)} %get-tuple-element.42), channel_id=1, source_target_pairs={{1,0},{2,1},{3,2},{4,3},{5,4},{6,5},{7,6},{9,8},{10,9},{11,10},{12... | collective-permute-start | bytes 491528 | tf_op jit(solution)/shard_map/ppermute | solution.py:228
  33.2 7.1 %collective-permute-start.9 = (f32[5,2,32,128]{3,2,1,0:T(8,128)S(1)}, f32[5,2,32,128]{3,2,1,0:T(8,128)S(1)}, u32[]{:S(2)}, u32[]{:S(2)}) collective-permute-start(f32[5,2,32,128]{3,2,1,0:T(8,128)S(1)} %get-tuple-element.38), channel_id=1, source_target_pairs={{0,8},{8,16},{16,24},{24,0},{1,9},{9,17},{17,25},{25,1},{2,10},{10... | collective-permute-start | bytes 491528 | tf_op jit(solution)/shard_map/ppermute | solution.py:203
  33.3 7.1 %collective-permute-start.10 = (f32[5,2,32,128]{3,2,1,0:T(8,128)S(1)}, f32[5,2,32,128]{3,2,1,0:T(8,128)S(1)}, u32[]{:S(2)}, u32[]{:S(2)}) collective-permute-start(f32[5,2,32,128]{3,2,1,0:T(8,128)S(1)} %get-tuple-element.39), channel_id=1, source_target_pairs={{0,16},{8,24},{16,0},{24,8},{1,17},{9,25},{17,1},{25,9},{2,18},{10... | collective-permute-start | bytes 491528 | tf_op jit(solution)/shard_map/ppermute | solution.py:203
  34.6 8.9 %collective-permute-start.11 = (f32[5,2,32,128]{3,2,1,0:T(8,128)S(1)}, f32[5,2,32,128]{3,2,1,0:T(8,128)S(1)}, u32[]{:S(2)}, u32[]{:S(2)}) collective-permute-start(f32[5,2,32,128]{3,2,1,0:T(8,128)S(1)} %get-tuple-element.40), channel_id=1, source_target_pairs={{0,24},{8,0},{16,8},{24,16},{1,25},{9,1},{17,9},{25,17},{2,26},{10... | collective-permute-start | bytes 491528 | tf_op jit(solution)/shard_map/ppermute | solution.py:203
where the time goes:
time: 45.4 us; the launch traced here: 45.2 us
  starting transfers between devices  19.6 us (43%)
  waiting for transfers between devices  17.6 us (39%)
  Pallas kernels  7.9 us (17%)
    ppermute x12, waiting for transfers between devices, exchange(): lax.ppermute(parts[k], 'az', [(i, (i + k) % group) for i in range(group)])  17.6 us
    ppermute x12, starting transfers between devices, exchange(): lax.ppermute(parts[k], 'az', [(i, (i + k) % group) for i in range(group)])  14 us
    ppermute x1, starting transfers between devices, substep(): parts.append(lax.ppermute(low, 'rad', down))  3.64 us
    pallas_call x2, Pallas kernels, azimuthal(): pl.pallas_call(functools.partial(azimuthal_kernel, starts, rows), out_sha...  3.25 us
    pallas_call x2, Pallas kernels, pack(): pl.pallas_call(functools.partial(pack_kernel, table, rows), out_shape=kin...  2.95 us
    ppermute x1, starting transfers between devices, substep(): parts.append(lax.ppermute(high, 'rad', up))  1.92 us
    pallas_call x1, Pallas kernels, radial(): pl.pallas_call(functools.partial(radial_kernel, places, rows), out_shape=...  1.64 us
  transfers between devices with their start and end apart: 14, of which 5 were waited for; matrix products, arithmetic and copies ran while one was open for 0% of the time, Pallas kernels for 9%

commit v1 on v0

--- a/solution.py
+++ b/solution.py
@@ -24,69 +24,72 @@
 
 def plan(rows, group):
     edges = [0, 1, rows - 2, rows - 1]
-    inner = [row for row in range(rows) if row not in edges]
-    first = edges + inner[: group - len(edges)]
-    rest = inner[group - len(edges):]
-    each = len(rest) // group
-    starts = [rest[device * each] for device in range(group)] if each else []
-    return first, starts, each
+    order = edges + [row for row in range(rows) if row not in edges]
+    lists = [order[start:start + group] for start in range(0, rows, group)]
+    count = len(lists) - len(lists) // 3
+    return [part for part in (lists[:count], lists[count:]) if part]
 
 
 def kept(array):
     return pltpu.with_memory_space_constraint(array, pltpu.VMEM)
 
 
-def pack_kernel(table, rows, fields, turned, *refs):
-    group = len(table)
-    results, rates, sems = (refs[:group], refs[group:-1], refs[-1])
-    here = lax.axis_index("az")
+def pack_kernel(lists, fields, *refs):
+    results, sems = (refs[:-1], refs[-1])
+    group, here = (len(results), lax.axis_index("az"))
     copies = []
     for place, result in enumerate(results):
-        rotated = [table[(device + place) % group] for device in range(group)]
-        source = fields.at[:, pl.ds(pick(rotated, here), result.shape[1])]
-        copies.append(pltpu.make_async_copy(source, result, sems.at[place]))
+        for step, table in enumerate(lists):
+            row = pick([table[(device + place) % group] for device in range(group)], here)
+            copies.append(
+                pltpu.make_async_copy(fields.at[:, row], result.at[:, step], sems.at[place, step])
+            )
     for copy in copies:
         copy.start()
-    if rates:
-        spread_rates(turned, rates[0], lax.axis_index("rad") * rows - 1)
     for copy in copies:
         copy.wait()
 
 
-def spread_rates(turned, result, below):
+def pack(fields, lists, group):
+    shape = (fields.shape[0], len(lists)) + fields.shape[2:]
+    return pl.pallas_call(
+        functools.partial(pack_kernel, lists),
+        out_shape=[pltpu.VMEM(shape, fields.dtype)] * group,
+        in_specs=[pl.BlockSpec(memory_space=pl.ANY)],
+        out_specs=[pl.BlockSpec(memory_space=pltpu.VMEM)] * group,
+        scratch_shapes=[pltpu.SemaphoreType.DMA((group, len(lists)))],
+        name="pack",
+    )(fields)
+
+
+def rates_kernel(rows, turned, result):
     columns = turned[...]
     place = lax.broadcasted_iota(jnp.int32, columns.shape, 1)
     inside = jnp.where(place < columns.shape[1] - 1, columns, 0.0)
+    below = lax.axis_index("rad") * rows - 1
     for row in range(result.shape[0]):
         column = jnp.sum(jnp.where(place == below + row, inside, 0.0), axis=1, keepdims=True)
         result[row] = jnp.broadcast_to(column, result.shape[1:])
 
 
-def pack(fields, radial_rate, table, count, with_rates):
-    group, rows = (len(table), fields.shape[1])
-    shape = (fields.shape[0], count) + fields.shape[2:]
-    kinds = [pltpu.VMEM(shape, fields.dtype)] * group
-    kinds += [pltpu.VMEM((rows + 1,) + fields.shape[2:], jnp.float32)] * with_rates
-    vmem = pl.BlockSpec(memory_space=pltpu.VMEM)
-    return pl.pallas_call(
-        functools.partial(pack_kernel, table, rows),
-        out_shape=kinds,
-        in_specs=[pl.BlockSpec(memory_space=pl.ANY), vmem if with_rates else pl.BlockSpec(memory_space=pl.ANY)],
-        out_specs=[vmem] * len(kinds),
-        scratch_shapes=[pltpu.SemaphoreType.DMA((group,))],
-        name="pack",
-    )(fields, radial_rate.T)
-
-
-def azimuthal_kernel(starts, rows, shift, fraction, *refs):
+def spread_rates(radial_rate, rows, width):
+    return pl.pallas_call(
+        functools.partial(rates_kernel, rows),
+        out_shape=pltpu.VMEM((rows + 1, radial_rate.shape[1], width), jnp.float32),
+        in_specs=[pl.BlockSpec(memory_space=pltpu.VMEM)],
+        out_specs=pl.BlockSpec(memory_space=pltpu.VMEM),
+        name="spread_rates",
+    )(radial_rate.T)
+
+
+def azimuthal_kernel(lists, rows, shift, fraction, *refs):
     group = len(refs) // 2
     parts, results = (refs[:group], refs[group:])
     fields, count, polar, width = parts[0].shape
     cycle = group * width
-    first = lax.axis_index("rad") * rows + pick(starts, lax.axis_index("az"))
     for step in range(count):
-        move = shift[first + step]
-        courant = fraction[first + step]
+        row = lax.axis_index("rad") * rows + pick(lists[step], lax.axis_index("az"))
+        move, courant = (shift[row], fraction[row])
         ahead = courant > 0.0
         weight = jnp.where(ahead, 0.5 * (1.0 - courant), -0.5 * (1.0 + courant))
         cells = jnp.concatenate(
@@ -107,11 +110,11 @@
             )
 
 
-def azimuthal(parts, starts, rows, shift, fraction):
+def azimuthal(parts, lists, rows, shift, fraction):
     vmem = pl.BlockSpec(memory_space=pltpu.VMEM)
     smem = pl.BlockSpec(memory_space=pltpu.SMEM)
     return pl.pallas_call(
-        functools.partial(azimuthal_kernel, starts, rows),
+        functools.partial(azimuthal_kernel, lists, rows),
         out_shape=[pltpu.VMEM(part.shape, part.dtype) for part in parts],
         in_specs=[smem, smem] + [vmem] * len(parts),
         out_specs=[vmem] * len(parts),
@@ -123,12 +126,12 @@
     count = len(places)
     parts, result, cells, done, sems = (refs[:count],) + refs[count:]
     here = lax.axis_index("az")
-    starts = [pick(place, here) for place in places]
+    starts = [[pick(table, here) for table in place] for place in places]
     copies = []
     for field in range(parts[0].shape[0]):
         for part, start in zip(parts, starts):
-            for step in range(part.shape[1]):
-                cells[field, start + step] = part[field, step]
+            for step, row in enumerate(start):
+                cells[field, row] = part[field, step]
         flow(cells.at[field], rates, done.at[field], rows)
         copies.append(pltpu.make_async_copy(done.at[field], result.at[field], sems.at[field]))
         copies[-1].start()
@@ -207,26 +210,24 @@
 def substep(fields, shift, fraction, radial_rate):
     rows = fields.shape[1]
     group, blocks = (lax.axis_size("az"), lax.axis_size("rad"))
-    first, starts, each = plan(rows, group)
-    sets = [(first, 1)] + ([(starts, each)] if each else [])
+    sets = plan(rows, group)
     cycles = []
-    for turn, (table, count) in enumerate(sets):
-        last = turn == len(sets) - 1
-        packed = pack(fields, radial_rate, table, count, last)
-        cycles.append(exchange(packed[:group], group))
-    rates = packed[group]
+    for lists in sets:
+        packed = pack(fields, lists, group)
+        cycles.append(exchange(packed, group))
     parts, places = ([], [])
-    for (table, count), cycle in zip(sets, cycles):
-        updated = azimuthal(cycle, table, rows, shift, fraction)
+    for lists, cycle in zip(sets, cycles):
+        updated = azimuthal(cycle, lists, rows, shift, fraction)
         parts += exchange(updated, group)
         for k in range(group):
-            places.append([2 + table[(i - k) % group] for i in range(group)])
+            places.append([[2 + table[(i - k) % group] for i in range(group)] for table in lists])
     low, high = edges(parts[:group])
     up = [(b, b + 1) for b in range(blocks - 1)]
     down = [(b, a) for a, b in up]
     parts.append(lax.ppermute(high, "rad", up))
     parts.append(lax.ppermute(low, "rad", down))
-    places += [[0] * group, [rows + 2] * group]
+    places += [[[0] * group, [1] * group], [[rows + 2] * group, [rows + 3] * group]]
+    rates = spread_rates(radial_rate, rows, fields.shape[3])
     return radial(parts, places, rates, rows)
 
 

time: 45.4 us -> 42.6 us (0.938)
  the two profiles are of different devices: /device:TPU:18 before, /device:TPU:20 now
where the time goes in v1:
time: 42.6 us; the launch traced here: 42.3 us
  starting transfers between devices  19.2 us (45%)
  waiting for transfers between devices  14.9 us (35%)
  Pallas kernels  8.07 us (19%)
    ppermute x12, waiting for transfers between devices, exchange(): lax.ppermute(parts[k], 'az', [(i, (i + k) % group) for i in range(group)])  14.9 us
    ppermute x12, starting transfers between devices, exchange(): lax.ppermute(parts[k], 'az', [(i, (i + k) % group) for i in range(group)])  13.6 us
    ppermute x1, starting transfers between devices, substep(): parts.append(lax.ppermute(low, 'rad', down))  3.64 us
    pallas_call x2, Pallas kernels, azimuthal(): pl.pallas_call(functools.partial(azimuthal_kernel, lists, rows), out_shap...  3.25 us
    pallas_call x2, Pallas kernels, pack(): pl.pallas_call(functools.partial(pack_kernel, lists), out_shape=[pltpu.VM...  2.28 us
    ppermute x1, starting transfers between devices, substep(): parts.append(lax.ppermute(high, 'rad', up))  1.92 us
    pallas_call x1, Pallas kernels, radial(): pl.pallas_call(functools.partial(radial_kernel, places, rows), out_shape=...  1.65 us
  transfers between devices with their start and end apart: 14, of which 7 were waited for; matrix products, arithmetic and copies ran while one was open for 0% of the time, Pallas kernels for 8%

profile of v1, /device:TPU:20, one launch (start us, length us, event | category | flops | bytes accessed | tf_op | source)
XLA Modules:
  0.0 42.3 jit_solution(11553897582840879308)
XLA Ops:
  0.0 1.2 %pack.2 = (f32[5,2,32,128]{3,2,1,0:T(8,128)S(1)}, f32[5,2,32,128]{3,2,1,0:T(8,128)S(1)}, f32[5,2,32,128]{3,2,1,0:T(8,128)S(1)}, f32[5,2,32,128]{3,2,1,0:T(8,128)S(1)}) custom-call(f32[5,12,32,128]{3,2,1,0:T(8,128)} %fields.3), custom_call_target="tpu_custom_call" | custom-call | tf_op jit(solution)/shard_map/pack/pallas_call | solution.py:55
  1.2 1.5 %collective-permute-start = (f32[5,2,32,128]{3,2,1,0:T(8,128)S(1)}, f32[5,2,32,128]{3,2,1,0:T(8,128)S(1)}, u32[]{:S(2)}, u32[]{:S(2)}) collective-permute-start(f32[5,2,32,128]{3,2,1,0:T(8,128)S(1)} %get-tuple-element.24), channel_id=1, source_target_pairs={{0,8},{8,16},{16,24},{24,0},{1,9},{9,17},{17,25},{25,1},{2,10},{10... | collective-permute-start | bytes 491528 | tf_op jit(solution)/shard_map/ppermute | solution.py:206
  3.3 1.4 %collective-permute-start.2 = (f32[5,2,32,128]{3,2,1,0:T(8,128)S(1)}, f32[5,2,32,128]{3,2,1,0:T(8,128)S(1)}, u32[]{:S(2)}, u32[]{:S(2)}) collective-permute-start(f32[5,2,32,128]{3,2,1,0:T(8,128)S(1)} %get-tuple-element.26), channel_id=1, source_target_pairs={{0,24},{8,0},{16,8},{24,16},{1,25},{9,1},{17,9},{25,17},{2,26},{10... | collective-permute-start | bytes 491528 | tf_op jit(solution)/shard_map/ppermute | solution.py:206
  4.7 4.6 %collective-permute-done.refs_1_ = f32[5,2,32,128]{3,2,1,0:T(8,128)S(1)} collective-permute-done((f32[5,2,32,128]{3,2,1,0:T(8,128)S(1)}, f32[5,2,32,128]{3,2,1,0:T(8,128)S(1)}, u32[]{:S(2)}, u32[]{:S(2)}) %collective-permute-start) | collective-permute-done | bytes 163872 | tf_op jit(solution)/shard_map/ppermute | solution.py:206
  9.3 2.3 %collective-permute-done.1.refs_2_ = f32[5,2,32,128]{3,2,1,0:T(8,128)S(1)} collective-permute-done((f32[5,2,32,128]{3,2,1,0:T(8,128)S(1)}, f32[5,2,32,128]{3,2,1,0:T(8,128)S(1)}, u32[]{:S(2)}, u32[]{:S(2)}) %collective-permute-start.1) | collective-permute-done | bytes 163872 | tf_op jit(solution)/shard_map/ppermute | solution.py:206
  11.7 1.9 %azimuthal.2 = (f32[5,2,32,128]{3,2,1,0:T(8,128)S(1)}, f32[5,2,32,128]{3,2,1,0:T(8,128)S(1)}, f32[5,2,32,128]{3,2,1,0:T(8,128)S(1)}, f32[5,2,32,128]{3,2,1,0:T(8,128)S(1)}) custom-call(s32[96]{0:T(128)} %shift.3, f32[96]{0:T(128)} %fraction.3, f32[5,2,32,128]{3,2,1,0:T(8,128)S(1)} %get-tuple-element.23.refs_0_, ...), custom_call_target="tpu_custom_call" | custom-call | tf_op jit(solution)/shard_map/azimuthal/pallas_call | solution.py:116
  13.6 0.8 %collective-permute-start.3 = (f32[5,2,32,128]{3,2,1,0:T(8,128)S(1)}, f32[5,2,32,128]{3,2,1,0:T(8,128)S(1)}, u32[]{:S(2)}, u32[]{:S(2)}) collective-permute-start(f32[5,2,32,128]{3,2,1,0:T(8,128)S(1)} %get-tuple-element.28), channel_id=1, source_target_pairs={{0,8},{8,16},{16,24},{24,0},{1,9},{9,17},{17,25},{25,1},{2,10},{10... | collective-permute-start | bytes 491528 | tf_op jit(solution)/shard_map/ppermute | solution.py:206
  14.4 1.5 %collective-permute-start.4 = (f32[5,2,32,128]{3,2,1,0:T(8,128)S(1)}, f32[5,2,32,128]{3,2,1,0:T(8,128)S(1)}, u32[]{:S(2)}, u32[]{:S(2)}) collective-permute-start(f32[5,2,32,128]{3,2,1,0:T(8,128)S(1)} %get-tuple-element.29), channel_id=1, source_target_pairs={{0,16},{8,24},{16,0},{24,8},{1,17},{9,25},{17,1},{25,9},{2,18},{10... | collective-permute-start | bytes 491528 | tf_op jit(solution)/shard_map/ppermute | solution.py:206
  15.9 1.2 %collective-permute-start.5 = (f32[5,2,32,128]{3,2,1,0:T(8,128)S(1)}, f32[5,2,32,128]{3,2,1,0:T(8,128)S(1)}, u32[]{:S(2)}, u32[]{:S(2)}) collective-permute-start(f32[5,2,32,128]{3,2,1,0:T(8,128)S(1)} %get-tuple-element.30), channel_id=1, source_target_pairs={{0,24},{8,0},{16,8},{24,16},{1,25},{9,1},{17,9},{25,17},{2,26},{10... | collective-permute-start | bytes 491528 | tf_op jit(solution)/shard_map/ppermute | solution.py:206
  17.2 1.0 %pack.3 = (f32[5,1,32,128]{3,2,1,0:T(8,128)S(1)}, f32[5,1,32,128]{3,2,1,0:T(8,128)S(1)}, f32[5,1,32,128]{3,2,1,0:T(8,128)S(1)}, f32[5,1,32,128]{3,2,1,0:T(8,128)S(1)}) custom-call(f32[5,12,32,128]{3,2,1,0:T(8,128)} %fields.3), custom_call_target="tpu_custom_call" | custom-call | tf_op jit(solution)/shard_map/pack/pallas_call | solution.py:55
  18.2 0.9 %collective-permute-start.6 = (f32[5,1,32,128]{3,2,1,0:T(8,128)S(1)}, f32[5,1,32,128]{3,2,1,0:T(8,128)S(1)}, u32[]{:S(2)}, u32[]{:S(2)}) collective-permute-start(f32[5,1,32,128]{3,2,1,0:T(8,128)S(1)} %get-tuple-element.32), channel_id=1, source_target_pairs={{0,8},{8,16},{16,24},{24,0},{1,9},{9,17},{17,25},{25,1},{2,10},{10... | collective-permute-start | bytes 245768 | tf_op jit(solution)/shard_map/ppermute | solution.py:206
  19.1 0.7 %collective-permute-start.7 = (f32[5,1,32,128]{3,2,1,0:T(8,128)S(1)}, f32[5,1,32,128]{3,2,1,0:T(8,128)S(1)}, u32[]{:S(2)}, u32[]{:S(2)}) collective-permute-start(f32[5,1,32,128]{3,2,1,0:T(8,128)S(1)} %get-tuple-element.33), channel_id=1, source_target_pairs={{0,16},{8,24},{16,0},{24,8},{1,17},{9,25},{17,1},{25,9},{2,18},{10... | collective-permute-start | bytes 245768 | tf_op jit(solution)/shard_map/ppermute | solution.py:206
  19.8 1.9 %collective-permute-done.3.refs_1_ = f32[5,2,32,128]{3,2,1,0:T(8,128)S(1)} collective-permute-done((f32[5,2,32,128]{3,2,1,0:T(8,128)S(1)}, f32[5,2,32,128]{3,2,1,0:T(8,128)S(1)}, u32[]{:S(2)}, u32[]{:S(2)}) %collective-permute-start.3) | collective-permute-done | bytes 163872 | tf_op jit(solution)/shard_map/ppermute | solution.py:206
  21.6 1.0 %collective-permute-start.8 = (f32[5,1,32,128]{3,2,1,0:T(8,128)S(1)}, f32[5,1,32,128]{3,2,1,0:T(8,128)S(1)}, u32[]{:S(2)}, u32[]{:S(2)}) collective-permute-start(f32[5,1,32,128]{3,2,1,0:T(8,128)S(1)} %get-tuple-element.34), channel_id=1, source_target_pairs={{0,24},{8,0},{16,8},{24,16},{1,25},{9,1},{17,9},{25,17},{2,26},{10... | collective-permute-start | bytes 245768 | tf_op jit(solution)/shard_map/ppermute | solution.py:206
  22.6 2.5 %collective-permute-done.4.refs_2_ = f32[5,2,32,128]{3,2,1,0:T(8,128)S(1)} collective-permute-done((f32[5,2,32,128]{3,2,1,0:T(8,128)S(1)}, f32[5,2,32,128]{3,2,1,0:T(8,128)S(1)}, u32[]{:S(2)}, u32[]{:S(2)}) %collective-permute-start.4) | collective-permute-done | bytes 163872 | tf_op jit(solution)/shard_map/ppermute | solution.py:206
  25.2 1.9 %collective-permute-start.12 = (f32[5,2,32,128]{3,2,1,0:T(8,128)S(1)}, f32[5,2,32,128]{3,2,1,0:T(8,128)S(1)}, u32[]{:S(2)}, u32[]{:S(2)}) collective-permute-start(f32[5,2,32,128]{3,2,1,0:T(8,128)S(1)} %get-tuple-element.39), channel_id=1, source_target_pairs={{0,1},{1,2},{2,3},{3,4},{4,5},{5,6},{6,7},{8,9},{9,10},{10,11},{11... | collective-permute-start | bytes 491528 | tf_op jit(solution)/shard_map/ppermute | solution.py:227
  27.1 3.6 %collective-permute-start.13 = (f32[5,2,32,128]{3,2,1,0:T(8,128)S(1)}, f32[5,2,32,128]{3,2,1,0:T(8,128)S(1)}, u32[]{:S(2)}, u32[]{:S(2)}) collective-permute-start(f32[5,2,32,128]{3,2,1,0:T(8,128)S(1)} %get-tuple-element.40), channel_id=1, source_target_pairs={{1,0},{2,1},{3,2},{4,3},{5,4},{6,5},{7,6},{9,8},{10,9},{11,10},{12... | collective-permute-start | bytes 491528 | tf_op jit(solution)/shard_map/ppermute | solution.py:228
  30.8 1.3 %azimuthal.3 = (f32[5,1,32,128]{3,2,1,0:T(8,128)S(1)}, f32[5,1,32,128]{3,2,1,0:T(8,128)S(1)}, f32[5,1,32,128]{3,2,1,0:T(8,128)S(1)}, f32[5,1,32,128]{3,2,1,0:T(8,128)S(1)}) custom-call(s32[96]{0:T(128)} %shift.3, f32[96]{0:T(128)} %fraction.3, f32[5,1,32,128]{3,2,1,0:T(8,128)S(1)} %get-tuple-element.31.refs_0_, ...), custom_call_target="tpu_custom_call" | custom-call | tf_op jit(solution)/shard_map/azimuthal/pallas_call | solution.py:116
  32.1 1.6 %collective-permute-start.9 = (f32[5,1,32,128]{3,2,1,0:T(8,128)S(1)}, f32[5,1,32,128]{3,2,1,0:T(8,128)S(1)}, u32[]{:S(2)}, u32[]{:S(2)}) collective-permute-start(f32[5,1,32,128]{3,2,1,0:T(8,128)S(1)} %get-tuple-element.36), channel_id=1, source_target_pairs={{0,8},{8,16},{16,24},{24,0},{1,9},{9,17},{17,25},{25,1},{2,10},{10... | collective-permute-start | bytes 245768 | tf_op jit(solution)/shard_map/ppermute | solution.py:206
  33.7 2.4 %collective-permute-start.10 = (f32[5,1,32,128]{3,2,1,0:T(8,128)S(1)}, f32[5,1,32,128]{3,2,1,0:T(8,128)S(1)}, u32[]{:S(2)}, u32[]{:S(2)}) collective-permute-start(f32[5,1,32,128]{3,2,1,0:T(8,128)S(1)} %get-tuple-element.37), channel_id=1, source_target_pairs={{0,16},{8,24},{16,0},{24,8},{1,17},{9,25},{17,1},{25,9},{2,18},{10... | collective-permute-start | bytes 245768 | tf_op jit(solution)/shard_map/ppermute | solution.py:206
  36.2 0.8 %spread_rates.1.rates = f32[13,32,128]{2,1,0:T(8,128)S(1)} custom-call(f32[32,96]{1,0:T(8,128)} %bitcast.1), custom_call_target="tpu_custom_call" | custom-call | tf_op jit(solution)/shard_map/spread_rates/pallas_call | solution.py:76
  37.0 1.4 %collective-permute-done.9.refs_5_ = f32[5,1,32,128]{3,2,1,0:T(8,128)S(1)} collective-permute-done((f32[5,1,32,128]{3,2,1,0:T(8,128)S(1)}, f32[5,1,32,128]{3,2,1,0:T(8,128)S(1)}, u32[]{:S(2)}, u32[]{:S(2)}) %collective-permute-start.9) | collective-permute-done | bytes 81952 | tf_op jit(solution)/shard_map/ppermute | solution.py:206
  38.5 1.5 %collective-permute-done.10.refs_6_ = f32[5,1,32,128]{3,2,1,0:T(8,128)S(1)} collective-permute-done((f32[5,1,32,128]{3,2,1,0:T(8,128)S(1)}, f32[5,1,32,128]{3,2,1,0:T(8,128)S(1)}, u32[]{:S(2)}, u32[]{:S(2)}) %collective-permute-start.10) | collective-permute-done | bytes 81952 | tf_op jit(solution)/shard_map/ppermute | solution.py:206
  40.6 1.6 %radial.1 = f32[5,12,32,128]{3,2,1,0:T(8,128)} custom-call(f32[13,32,128]{2,1,0:T(8,128)S(1)} %spread_rates.1.rates, f32[5,2,32,128]{3,2,1,0:T(8,128)S(1)} %get-tuple-element.27.refs_0_, f32[5,2,32,128]{3,2,1,0:T(8,128)S(1)} %collective-permute-done.3.refs_1_, f32[5,2,32,128]{3,2,1,0:T(8,128)S(1)} %collective-permute-done.4.refs_2_, ...), custom_call_target="tpu_custom_call" | custom-call | tf_op jit(solution)/shard_map/radial/pallas_call | solution.py:165
  (11 shorter events, 1.3 us)
Async XLA Ops:
  1.2 8.1 %collective-permute-start = (f32[5,2,32,128]{3,2,1,0:T(8,128)S(1)}, f32[5,2,32,128]{3,2,1,0:T(8,128)S(1)}, u32[]{:S(2)}, u32[]{:S(2)}) collective-permute-start(f32[5,2,32,128]{3,2,1,0:T(8,128)S(1)} %get-tuple-element.24), channel_id=1, source_target_pairs={{0,8},{8,16},{16,24},{24,0},{1,9},{9,17},{17,25},{25,1},{2,10},{10... | collective-permute-start | bytes 491528 | tf_op jit(solution)/shard_map/ppermute | solution.py:206
  2.8 8.9 %collective-permute-start.1 = (f32[5,2,32,128]{3,2,1,0:T(8,128)S(1)}, f32[5,2,32,128]{3,2,1,0:T(8,128)S(1)}, u32[]{:S(2)}, u32[]{:S(2)}) collective-permute-start(f32[5,2,32,128]{3,2,1,0:T(8,128)S(1)} %get-tuple-element.25), channel_id=1, source_target_pairs={{0,16},{8,24},{16,0},{24,8},{1,17},{9,25},{17,1},{25,9},{2,18},{10... | collective-permute-start | bytes 491528 | tf_op jit(solution)/shard_map/ppermute | solution.py:206
  3.3 8.4 %collective-permute-start.2 = (f32[5,2,32,128]{3,2,1,0:T(8,128)S(1)}, f32[5,2,32,128]{3,2,1,0:T(8,128)S(1)}, u32[]{:S(2)}, u32[]{:S(2)}) collective-permute-start(f32[5,2,32,128]{3,2,1,0:T(8,128)S(1)} %get-tuple-element.26), channel_id=1, source_target_pairs={{0,24},{8,0},{16,8},{24,16},{1,25},{9,1},{17,9},{25,17},{2,26},{10... | collective-permute-start | bytes 491528 | tf_op jit(solution)/shard_map/ppermute | solution.py:206
  13.6 8.1 %collective-permute-start.3 = (f32[5,2,32,128]{3,2,1,0:T(8,128)S(1)}, f32[5,2,32,128]{3,2,1,0:T(8,128)S(1)}, u32[]{:S(2)}, u32[]{:S(2)}) collective-permute-start(f32[5,2,32,128]{3,2,1,0:T(8,128)S(1)} %get-tuple-element.28), channel_id=1, source_target_pairs={{0,8},{8,16},{16,24},{24,0},{1,9},{9,17},{17,25},{25,1},{2,10},{10... | collective-permute-start | bytes 491528 | tf_op jit(solution)/shard_map/ppermute | solution.py:206
  14.4 10.7 %collective-permute-start.4 = (f32[5,2,32,128]{3,2,1,0:T(8,128)S(1)}, f32[5,2,32,128]{3,2,1,0:T(8,128)S(1)}, u32[]{:S(2)}, u32[]{:S(2)}) collective-permute-start(f32[5,2,32,128]{3,2,1,0:T(8,128)S(1)} %get-tuple-element.29), channel_id=1, source_target_pairs={{0,16},{8,24},{16,0},{24,8},{1,17},{9,25},{17,1},{25,9},{2,18},{10... | collective-permute-start | bytes 491528 | tf_op jit(solution)/shard_map/ppermute | solution.py:206
  15.9 9.2 %collective-permute-start.5 = (f32[5,2,32,128]{3,2,1,0:T(8,128)S(1)}, f32[5,2,32,128]{3,2,1,0:T(8,128)S(1)}, u32[]{:S(2)}, u32[]{:S(2)}) collective-permute-start(f32[5,2,32,128]{3,2,1,0:T(8,128)S(1)} %get-tuple-element.30), channel_id=1, source_target_pairs={{0,24},{8,0},{16,8},{24,16},{1,25},{9,1},{17,9},{25,17},{2,26},{10... | collective-permute-start | bytes 491528 | tf_op jit(solution)/shard_map/ppermute | solution.py:206
  18.2 12.5 %collective-permute-start.6 = (f32[5,1,32,128]{3,2,1,0:T(8,128)S(1)}, f32[5,1,32,128]{3,2,1,0:T(8,128)S(1)}, u32[]{:S(2)}, u32[]{:S(2)}) collective-permute-start(f32[5,1,32,128]{3,2,1,0:T(8,128)S(1)} %get-tuple-element.32), channel_id=1, source_target_pairs={{0,8},{8,16},{16,24},{24,0},{1,9},{9,17},{17,25},{25,1},{2,10},{10... | collective-permute-start | bytes 245768 | tf_op jit(solution)/shard_map/ppermute | solution.py:206
  19.1 11.7 %collective-permute-start.7 = (f32[5,1,32,128]{3,2,1,0:T(8,128)S(1)}, f32[5,1,32,128]{3,2,1,0:T(8,128)S(1)}, u32[]{:S(2)}, u32[]{:S(2)}) collective-permute-start(f32[5,1,32,128]{3,2,1,0:T(8,128)S(1)} %get-tuple-element.33), channel_id=1, source_target_pairs={{0,16},{8,24},{16,0},{24,8},{1,17},{9,25},{17,1},{25,9},{2,18},{10... | collective-permute-start | bytes 245768 | tf_op jit(solution)/shard_map/ppermute | solution.py:206
  21.6 9.1 %collective-permute-start.8 = (f32[5,1,32,128]{3,2,1,0:T(8,128)S(1)}, f32[5,1,32,128]{3,2,1,0:T(8,128)S(1)}, u32[]{:S(2)}, u32[]{:S(2)}) collective-permute-start(f32[5,1,32,128]{3,2,1,0:T(8,128)S(1)} %get-tuple-element.34), channel_id=1, source_target_pairs={{0,24},{8,0},{16,8},{24,16},{1,25},{9,1},{17,9},{25,17},{2,26},{10... | collective-permute-start | bytes 245768 | tf_op jit(solution)/shard_map/ppermute | solution.py:206
  25.2 15.5 %collective-permute-start.12 = (f32[5,2,32,128]{3,2,1,0:T(8,128)S(1)}, f32[5,2,32,128]{3,2,1,0:T(8,128)S(1)}, u32[]{:S(2)}, u32[]{:S(2)}) collective-permute-start(f32[5,2,32,128]{3,2,1,0:T(8,128)S(1)} %get-tuple-element.39), channel_id=1, source_target_pairs={{0,1},{1,2},{2,3},{3,4},{4,5},{5,6},{6,7},{8,9},{9,10},{10,11},{11... | collective-permute-start | bytes 491528 | tf_op jit(solution)/shard_map/ppermute | solution.py:227
  27.1 13.5 %collective-permute-start.13 = (f32[5,2,32,128]{3,2,1,0:T(8,128)S(1)}, f32[5,2,32,128]{3,2,1,0:T(8,128)S(1)}, u32[]{:S(2)}, u32[]{:S(2)}) collective-permute-start(f32[5,2,32,128]{3,2,1,0:T(8,128)S(1)} %get-tuple-element.40), channel_id=1, source_target_pairs={{1,0},{2,1},{3,2},{4,3},{5,4},{6,5},{7,6},{9,8},{10,9},{11,10},{12... | collective-permute-start | bytes 491528 | tf_op jit(solution)/shard_map/ppermute | solution.py:228
  32.1 6.4 %collective-permute-start.9 = (f32[5,1,32,128]{3,2,1,0:T(8,128)S(1)}, f32[5,1,32,128]{3,2,1,0:T(8,128)S(1)}, u32[]{:S(2)}, u32[]{:S(2)}) collective-permute-start(f32[5,1,32,128]{3,2,1,0:T(8,128)S(1)} %get-tuple-element.36), channel_id=1, source_target_pairs={{0,8},{8,16},{16,24},{24,0},{1,9},{9,17},{17,25},{25,1},{2,10},{10... | collective-permute-start | bytes 245768 | tf_op jit(solution)/shard_map/ppermute | solution.py:206
  33.7 6.2 %collective-permute-start.10 = (f32[5,1,32,128]{3,2,1,0:T(8,128)S(1)}, f32[5,1,32,128]{3,2,1,0:T(8,128)S(1)}, u32[]{:S(2)}, u32[]{:S(2)}) collective-permute-start(f32[5,1,32,128]{3,2,1,0:T(8,128)S(1)} %get-tuple-element.37), channel_id=1, source_target_pairs={{0,16},{8,24},{16,0},{24,8},{1,17},{9,25},{17,1},{25,9},{2,18},{10... | collective-permute-start | bytes 245768 | tf_op jit(solution)/shard_map/ppermute | solution.py:206
  36.2 4.4 %collective-permute-start.11 = (f32[5,1,32,128]{3,2,1,0:T(8,128)S(1)}, f32[5,1,32,128]{3,2,1,0:T(8,128)S(1)}, u32[]{:S(2)}, u32[]{:S(2)}) collective-permute-start(f32[5,1,32,128]{3,2,1,0:T(8,128)S(1)} %get-tuple-element.38), channel_id=1, source_target_pairs={{0,24},{8,0},{16,8},{24,16},{1,25},{9,1},{17,9},{25,17},{2,26},{10... | collective-permute-start | bytes 245768 | tf_op jit(solution)/shard_map/ppermute | solution.py:206

commit v2 on v1

--- a/solution.py
+++ b/solution.py
@@ -26,40 +26,47 @@
     edges = [0, 1, rows - 2, rows - 1]
     order = edges + [row for row in range(rows) if row not in edges]
     lists = [order[start:start + group] for start in range(0, rows, group)]
-    count = len(lists) - len(lists) // 3
-    return [part for part in (lists[:count], lists[count:]) if part]
+    return [part for part in (lists[:1], lists[1:]) if part]
 
 
 def kept(array):
     return pltpu.with_memory_space_constraint(array, pltpu.VMEM)
 
 
-def pack_kernel(lists, fields, *refs):
+def pack_kernel(sets, fields, *refs):
     results, sems = (refs[:-1], refs[-1])
-    group, here = (len(results), lax.axis_index("az"))
+    group, here = (len(results) // len(sets), lax.axis_index("az"))
     copies = []
-    for place, result in enumerate(results):
-        for step, table in enumerate(lists):
-            row = pick([table[(device + place) % group] for device in range(group)], here)
-            copies.append(
-                pltpu.make_async_copy(fields.at[:, row], result.at[:, step], sems.at[place, step])
-            )
+    for turn, lists in enumerate(sets):
+        for place in range(group):
+            result = results[turn * group + place]
+            for step, table in enumerate(lists):
+                row = pick([table[(device + place) % group] for device in range(group)], here)
+                sem = sems.at[turn, place, step]
+                copies.append(
+                    pltpu.make_async_copy(fields.at[:, row], result.at[:, step], sem)
+                )
     for copy in copies:
         copy.start()
     for copy in copies:
         copy.wait()
 
 
-def pack(fields, lists, group):
-    shape = (fields.shape[0], len(lists)) + fields.shape[2:]
-    return pl.pallas_call(
-        functools.partial(pack_kernel, lists),
-        out_shape=[pltpu.VMEM(shape, fields.dtype)] * group,
+def pack(fields, sets, group):
+    kinds = []
+    for lists in sets:
+        shape = (fields.shape[0], len(lists)) + fields.shape[2:]
+        kinds += [pltpu.VMEM(shape, fields.dtype)] * group
+    longest = max(len(lists) for lists in sets)
+    packed = pl.pallas_call(
+        functools.partial(pack_kernel, sets),
+        out_shape=kinds,
         in_specs=[pl.BlockSpec(memory_space=pl.ANY)],
-        out_specs=[pl.BlockSpec(memory_space=pltpu.VMEM)] * group,
-        scratch_shapes=[pltpu.SemaphoreType.DMA((group, len(lists)))],
+        out_specs=[pl.BlockSpec(memory_space=pltpu.VMEM)] * len(kinds),
+        scratch_shapes=[pltpu.SemaphoreType.DMA((len(sets), group, longest))],
         name="pack",
     )(fields)
+    return [packed[turn * group:(turn + 1) * group] for turn in range(len(sets))]
 
 
 def rates_kernel(rows, turned, result):
@@ -211,10 +218,8 @@
     rows = fields.shape[1]
     group, blocks = (lax.axis_size("az"), lax.axis_size("rad"))
     sets = plan(rows, group)
-    cycles = []
-    for lists in sets:
-        packed = pack(fields, lists, group)
-        cycles.append(exchange(packed, group))
+    packed = pack(fields, sets, group)
+    cycles = [exchange(each, group) for each in packed]
     parts, places = ([], [])
     for lists, cycle in zip(sets, cycles):
         updated = azimuthal(cycle, lists, rows, shift, fraction)

time: 42.6 us -> 37.4 us (0.88)
  the two profiles are of different devices: /device:TPU:20 before, /device:TPU:1 now
where the time goes in v2:
time: 37.4 us; the launch traced here: 37.1 us
  starting transfers between devices  21.1 us (56%)
  waiting for transfers between devices  8.73 us (23%)
  Pallas kernels  7.2 us (19%)
    ppermute x12, starting transfers between devices, exchange(): lax.ppermute(parts[k], 'az', [(i, (i + k) % group) for i in range(group)])  12.6 us
    ppermute x1, starting transfers between devices, substep(): parts.append(lax.ppermute(high, 'rad', up))  6.57 us
    ppermute x12, waiting for transfers between devices, exchange(): lax.ppermute(parts[k], 'az', [(i, (i + k) % group) for i in range(group)])  4.91 us
    ppermute x1, waiting for transfers between devices, substep(): parts.append(lax.ppermute(low, 'rad', down))  3.82 us
    pallas_call x2, Pallas kernels, azimuthal(): pl.pallas_call(functools.partial(azimuthal_kernel, lists, rows), out_shap...  3.25 us
    ppermute x1, starting transfers between devices, substep(): parts.append(lax.ppermute(low, 'rad', down))  1.92 us
    pallas_call x1, Pallas kernels, radial(): pl.pallas_call(functools.partial(radial_kernel, places, rows), out_shape=...  1.64 us
    pallas_call x1, Pallas kernels, pack(): pl.pallas_call(functools.partial(pack_kernel, sets), out_shape=kinds, in_...  1.41 us
  transfers between devices with their start and end apart: 14, of which 2 were waited for; matrix products, arithmetic and copies ran while one was open for 0% of the time, Pallas kernels for 11%

profile of v2, /device:TPU:1, one launch (start us, length us, event | category | flops | bytes accessed | tf_op | source)
XLA Modules:
  0.0 37.1 jit_solution(15126178690976242795)
XLA Ops:
  0.0 1.4 %pack.1 = (f32[5,1,32,128]{3,2,1,0:T(8,128)S(1)}, f32[5,1,32,128]{3,2,1,0:T(8,128)S(1)}, f32[5,1,32,128]{3,2,1,0:T(8,128)S(1)}, f32[5,1,32,128]{3,2,1,0:T(8,128)...) custom-call(f32[5,12,32,128]{3,2,1,0:T(8,128)} %fields.1), custom_call_target="tpu_custom_call" | custom-call | tf_op jit(solution)/shard_map/pack/pallas_call | solution.py:61
  1.4 2.1 %collective-permute-start = (f32[5,1,32,128]{3,2,1,0:T(8,128)S(1)}, f32[5,1,32,128]{3,2,1,0:T(8,128)S(1)}, u32[]{:S(2)}, u32[]{:S(2)}) collective-permute-start(f32[5,1,32,128]{3,2,1,0:T(8,128)S(1)} %get-tuple-element.24), channel_id=1, source_target_pairs={{0,8},{8,16},{16,24},{24,0},{1,9},{9,17},{17,25},{25,1},{2,10},{10... | collective-permute-start | bytes 245768 | tf_op jit(solution)/shard_map/ppermute | solution.py:213
  3.5 1.2 %collective-permute-start.6 = (f32[5,2,32,128]{3,2,1,0:T(8,128)S(1)}, f32[5,2,32,128]{3,2,1,0:T(8,128)S(1)}, u32[]{:S(2)}, u32[]{:S(2)}) collective-permute-start(f32[5,2,32,128]{3,2,1,0:T(8,128)S(1)} %get-tuple-element.32), channel_id=1, source_target_pairs={{0,8},{8,16},{16,24},{24,0},{1,9},{9,17},{17,25},{25,1},{2,10},{10... | collective-permute-start | bytes 491528 | tf_op jit(solution)/shard_map/ppermute | solution.py:213
  4.7 0.1 collective-permute-start.1
  4.8 2.3 %collective-permute-start.2 = (f32[5,1,32,128]{3,2,1,0:T(8,128)S(1)}, f32[5,1,32,128]{3,2,1,0:T(8,128)S(1)}, u32[]{:S(2)}, u32[]{:S(2)}) collective-permute-start(f32[5,1,32,128]{3,2,1,0:T(8,128)S(1)} %get-tuple-element.26), channel_id=1, source_target_pairs={{0,24},{8,0},{16,8},{24,16},{1,25},{9,1},{17,9},{25,17},{2,26},{10... | collective-permute-start | bytes 245768 | tf_op jit(solution)/shard_map/ppermute | solution.py:213
  7.1 0.2 collective-permute-start.7
  7.3 0.0 collective-permute-done.refs_1_
  7.3 0.4 %collective-permute-start.8 = (f32[5,2,32,128]{3,2,1,0:T(8,128)S(1)}, f32[5,2,32,128]{3,2,1,0:T(8,128)S(1)}, u32[]{:S(2)}, u32[]{:S(2)}) collective-permute-start(f32[5,2,32,128]{3,2,1,0:T(8,128)S(1)} %get-tuple-element.34), channel_id=1, source_target_pairs={{0,24},{8,0},{16,8},{24,16},{1,25},{9,1},{17,9},{25,17},{2,26},{10... | collective-permute-start | bytes 491528 | tf_op jit(solution)/shard_map/ppermute | solution.py:213
  7.7 4.9 %collective-permute-done.1.refs_2_ = f32[5,1,32,128]{3,2,1,0:T(8,128)S(1)} collective-permute-done((f32[5,1,32,128]{3,2,1,0:T(8,128)S(1)}, f32[5,1,32,128]{3,2,1,0:T(8,128)S(1)}, u32[]{:S(2)}, u32[]{:S(2)}) %collective-permute-start.1) | collective-permute-done | bytes 81952 | tf_op jit(solution)/shard_map/ppermute | solution.py:213
  12.6 0.0 collective-permute-done.2.refs_3_
  12.6 1.3 %azimuthal.2 = (f32[5,1,32,128]{3,2,1,0:T(8,128)S(1)}, f32[5,1,32,128]{3,2,1,0:T(8,128)S(1)}, f32[5,1,32,128]{3,2,1,0:T(8,128)S(1)}, f32[5,1,32,128]{3,2,1,0:T(8,128)S(1)}) custom-call(s32[96]{0:T(128)} %shift.3, f32[96]{0:T(128)} %fraction.3, f32[5,1,32,128]{3,2,1,0:T(8,128)S(1)} %get-tuple-element.23.refs_0_, ...), custom_call_target="tpu_custom_call" | custom-call | tf_op jit(solution)/shard_map/azimuthal/pallas_call | solution.py:123
  14.0 0.2 collective-permute-start.3
  14.1 1.2 %collective-permute-start.4 = (f32[5,1,32,128]{3,2,1,0:T(8,128)S(1)}, f32[5,1,32,128]{3,2,1,0:T(8,128)S(1)}, u32[]{:S(2)}, u32[]{:S(2)}) collective-permute-start(f32[5,1,32,128]{3,2,1,0:T(8,128)S(1)} %get-tuple-element.29), channel_id=1, source_target_pairs={{0,16},{8,24},{16,0},{24,8},{1,17},{9,25},{17,1},{25,9},{2,18},{10... | collective-permute-start | bytes 245768 | tf_op jit(solution)/shard_map/ppermute | solution.py:213
  15.4 2.3 %collective-permute-start.5 = (f32[5,1,32,128]{3,2,1,0:T(8,128)S(1)}, f32[5,1,32,128]{3,2,1,0:T(8,128)S(1)}, u32[]{:S(2)}, u32[]{:S(2)}) collective-permute-start(f32[5,1,32,128]{3,2,1,0:T(8,128)S(1)} %get-tuple-element.30), channel_id=1, source_target_pairs={{0,24},{8,0},{16,8},{24,16},{1,25},{9,1},{17,9},{25,17},{2,26},{10... | collective-permute-start | bytes 245768 | tf_op jit(solution)/shard_map/ppermute | solution.py:213
  17.7 1.9 %azimuthal.3 = (f32[5,2,32,128]{3,2,1,0:T(8,128)S(1)}, f32[5,2,32,128]{3,2,1,0:T(8,128)S(1)}, f32[5,2,32,128]{3,2,1,0:T(8,128)S(1)}, f32[5,2,32,128]{3,2,1,0:T(8,128)S(1)}) custom-call(s32[96]{0:T(128)} %shift.3, f32[96]{0:T(128)} %fraction.3, f32[5,2,32,128]{3,2,1,0:T(8,128)S(1)} %get-tuple-element.31.refs_0_, ...), custom_call_target="tpu_custom_call" | custom-call | tf_op jit(solution)/shard_map/azimuthal/pallas_call | solution.py:123
  19.6 0.1 collective-permute-start.9
  19.7 1.2 %collective-permute-start.10 = (f32[5,2,32,128]{3,2,1,0:T(8,128)S(1)}, f32[5,2,32,128]{3,2,1,0:T(8,128)S(1)}, u32[]{:S(2)}, u32[]{:S(2)}) collective-permute-start(f32[5,2,32,128]{3,2,1,0:T(8,128)S(1)} %get-tuple-element.37), channel_id=1, source_target_pairs={{0,16},{8,24},{16,0},{24,8},{1,17},{9,25},{17,1},{25,9},{2,18},{10... | collective-permute-start | bytes 491528 | tf_op jit(solution)/shard_map/ppermute | solution.py:213
  20.9 1.4 %collective-permute-start.11 = (f32[5,2,32,128]{3,2,1,0:T(8,128)S(1)}, f32[5,2,32,128]{3,2,1,0:T(8,128)S(1)}, u32[]{:S(2)}, u32[]{:S(2)}) collective-permute-start(f32[5,2,32,128]{3,2,1,0:T(8,128)S(1)} %get-tuple-element.38), channel_id=1, source_target_pairs={{0,24},{8,0},{16,8},{24,16},{1,25},{9,1},{17,9},{25,17},{2,26},{10... | collective-permute-start | bytes 491528 | tf_op jit(solution)/shard_map/ppermute | solution.py:213
  22.2 0.1 edges.1
  22.3 6.6 %collective-permute-start.12 = (f32[5,2,32,128]{3,2,1,0:T(8,128)S(1)}, f32[5,2,32,128]{3,2,1,0:T(8,128)S(1)}, u32[]{:S(2)}, u32[]{:S(2)}) collective-permute-start(f32[5,2,32,128]{3,2,1,0:T(8,128)S(1)} %get-tuple-element.39), channel_id=1, source_target_pairs={{0,1},{1,2},{2,3},{3,4},{4,5},{5,6},{6,7},{8,9},{9,10},{10,11},{11... | collective-permute-start | bytes 491528 | tf_op jit(solution)/shard_map/ppermute | solution.py:232
  28.9 1.9 %collective-permute-start.13 = (f32[5,2,32,128]{3,2,1,0:T(8,128)S(1)}, f32[5,2,32,128]{3,2,1,0:T(8,128)S(1)}, u32[]{:S(2)}, u32[]{:S(2)}) collective-permute-start(f32[5,2,32,128]{3,2,1,0:T(8,128)S(1)} %get-tuple-element.40), channel_id=1, source_target_pairs={{1,0},{2,1},{3,2},{4,3},{5,4},{6,5},{7,6},{9,8},{10,9},{11,10},{12... | collective-permute-start | bytes 491528 | tf_op jit(solution)/shard_map/ppermute | solution.py:233
  30.8 0.8 %spread_rates.1.rates = f32[13,32,128]{2,1,0:T(8,128)S(1)} custom-call(f32[32,96]{1,0:T(8,128)} %bitcast.1), custom_call_target="tpu_custom_call" | custom-call | tf_op jit(solution)/shard_map/spread_rates/pallas_call | solution.py:83
  31.7 3.8 %collective-permute-done.13.refs_9_ = f32[5,2,32,128]{3,2,1,0:T(8,128)S(1)} collective-permute-done((f32[5,2,32,128]{3,2,1,0:T(8,128)S(1)}, f32[5,2,32,128]{3,2,1,0:T(8,128)S(1)}, u32[]{:S(2)}, u32[]{:S(2)}) %collective-permute-start.13) | collective-permute-done | bytes 163872 | tf_op jit(solution)/shard_map/ppermute | solution.py:233
  35.5 1.6 %radial.1 = f32[5,12,32,128]{3,2,1,0:T(8,128)} custom-call(f32[13,32,128]{2,1,0:T(8,128)S(1)} %spread_rates.1.rates, f32[5,1,32,128]{3,2,1,0:T(8,128)S(1)} %get-tuple-element.27.refs_0_, f32[5,1,32,128]{3,2,1,0:T(8,128)S(1)} %collective-permute-done.3.refs_1_, f32[5,1,32,128]{3,2,1,0:T(8,128)S(1)} %collective-permute-done.4.refs_2_, ...), custom_call_target="tpu_custom_call" | custom-call | tf_op jit(solution)/shard_map/radial/pallas_call | solution.py:172
  (10 shorter events, 0.0 us)
Async XLA Ops:
  1.4 5.9 %collective-permute-start = (f32[5,1,32,128]{3,2,1,0:T(8,128)S(1)}, f32[5,1,32,128]{3,2,1,0:T(8,128)S(1)}, u32[]{:S(2)}, u32[]{:S(2)}) collective-permute-start(f32[5,1,32,128]{3,2,1,0:T(8,128)S(1)} %get-tuple-element.24), channel_id=1, source_target_pairs={{0,8},{8,16},{16,24},{24,0},{1,9},{9,17},{17,25},{25,1},{2,10},{10... | collective-permute-start | bytes 245768 | tf_op jit(solution)/shard_map/ppermute | solution.py:213
  3.5 11.9 %collective-permute-start.6 = (f32[5,2,32,128]{3,2,1,0:T(8,128)S(1)}, f32[5,2,32,128]{3,2,1,0:T(8,128)S(1)}, u32[]{:S(2)}, u32[]{:S(2)}) collective-permute-start(f32[5,2,32,128]{3,2,1,0:T(8,128)S(1)} %get-tuple-element.32), channel_id=1, source_target_pairs={{0,8},{8,16},{16,24},{24,0},{1,9},{9,17},{17,25},{25,1},{2,10},{10... | collective-permute-start | bytes 491528 | tf_op jit(solution)/shard_map/ppermute | solution.py:213
  4.7 7.9 %collective-permute-start.1 = (f32[5,1,32,128]{3,2,1,0:T(8,128)S(1)}, f32[5,1,32,128]{3,2,1,0:T(8,128)S(1)}, u32[]{:S(2)}, u32[]{:S(2)}) collective-permute-start(f32[5,1,32,128]{3,2,1,0:T(8,128)S(1)} %get-tuple-element.25), channel_id=1, source_target_pairs={{0,16},{8,24},{16,0},{24,8},{1,17},{9,25},{17,1},{25,9},{2,18},{10... | collective-permute-start | bytes 245768 | tf_op jit(solution)/shard_map/ppermute | solution.py:213
  4.8 7.8 %collective-permute-start.2 = (f32[5,1,32,128]{3,2,1,0:T(8,128)S(1)}, f32[5,1,32,128]{3,2,1,0:T(8,128)S(1)}, u32[]{:S(2)}, u32[]{:S(2)}) collective-permute-start(f32[5,1,32,128]{3,2,1,0:T(8,128)S(1)} %get-tuple-element.26), channel_id=1, source_target_pairs={{0,24},{8,0},{16,8},{24,16},{1,25},{9,1},{17,9},{25,17},{2,26},{10... | collective-permute-start | bytes 245768 | tf_op jit(solution)/shard_map/ppermute | solution.py:213
  7.1 10.6 %collective-permute-start.7 = (f32[5,2,32,128]{3,2,1,0:T(8,128)S(1)}, f32[5,2,32,128]{3,2,1,0:T(8,128)S(1)}, u32[]{:S(2)}, u32[]{:S(2)}) collective-permute-start(f32[5,2,32,128]{3,2,1,0:T(8,128)S(1)} %get-tuple-element.33), channel_id=1, source_target_pairs={{0,16},{8,24},{16,0},{24,8},{1,17},{9,25},{17,1},{25,9},{2,18},{10... | collective-permute-start | bytes 491528 | tf_op jit(solution)/shard_map/ppermute | solution.py:213
  7.3 10.3 %collective-permute-start.8 = (f32[5,2,32,128]{3,2,1,0:T(8,128)S(1)}, f32[5,2,32,128]{3,2,1,0:T(8,128)S(1)}, u32[]{:S(2)}, u32[]{:S(2)}) collective-permute-start(f32[5,2,32,128]{3,2,1,0:T(8,128)S(1)} %get-tuple-element.34), channel_id=1, source_target_pairs={{0,24},{8,0},{16,8},{24,16},{1,25},{9,1},{17,9},{25,17},{2,26},{10... | collective-permute-start | bytes 491528 | tf_op jit(solution)/shard_map/ppermute | solution.py:213
  14.0 6.9 %collective-permute-start.3 = (f32[5,1,32,128]{3,2,1,0:T(8,128)S(1)}, f32[5,1,32,128]{3,2,1,0:T(8,128)S(1)}, u32[]{:S(2)}, u32[]{:S(2)}) collective-permute-start(f32[5,1,32,128]{3,2,1,0:T(8,128)S(1)} %get-tuple-element.28), channel_id=1, source_target_pairs={{0,8},{8,16},{16,24},{24,0},{1,9},{9,17},{17,25},{25,1},{2,10},{10... | collective-permute-start | bytes 245768 | tf_op jit(solution)/shard_map/ppermute | solution.py:213
  14.1 8.1 %collective-permute-start.4 = (f32[5,1,32,128]{3,2,1,0:T(8,128)S(1)}, f32[5,1,32,128]{3,2,1,0:T(8,128)S(1)}, u32[]{:S(2)}, u32[]{:S(2)}) collective-permute-start(f32[5,1,32,128]{3,2,1,0:T(8,128)S(1)} %get-tuple-element.29), channel_id=1, source_target_pairs={{0,16},{8,24},{16,0},{24,8},{1,17},{9,25},{17,1},{25,9},{2,18},{10... | collective-permute-start | bytes 245768 | tf_op jit(solution)/shard_map/ppermute | solution.py:213
  15.4 6.8 %collective-permute-start.5 = (f32[5,1,32,128]{3,2,1,0:T(8,128)S(1)}, f32[5,1,32,128]{3,2,1,0:T(8,128)S(1)}, u32[]{:S(2)}, u32[]{:S(2)}) collective-permute-start(f32[5,1,32,128]{3,2,1,0:T(8,128)S(1)} %get-tuple-element.30), channel_id=1, source_target_pairs={{0,24},{8,0},{16,8},{24,16},{1,25},{9,1},{17,9},{25,17},{2,26},{10... | collective-permute-start | bytes 245768 | tf_op jit(solution)/shard_map/ppermute | solution.py:213
  19.6 12.0 %collective-permute-start.9 = (f32[5,2,32,128]{3,2,1,0:T(8,128)S(1)}, f32[5,2,32,128]{3,2,1,0:T(8,128)S(1)}, u32[]{:S(2)}, u32[]{:S(2)}) collective-permute-start(f32[5,2,32,128]{3,2,1,0:T(8,128)S(1)} %get-tuple-element.36), channel_id=1, source_target_pairs={{0,8},{8,16},{16,24},{24,0},{1,9},{9,17},{17,25},{25,1},{2,10},{10... | collective-permute-start | bytes 491528 | tf_op jit(solution)/shard_map/ppermute | solution.py:213
  19.7 12.0 %collective-permute-start.10 = (f32[5,2,32,128]{3,2,1,0:T(8,128)S(1)}, f32[5,2,32,128]{3,2,1,0:T(8,128)S(1)}, u32[]{:S(2)}, u32[]{:S(2)}) collective-permute-start(f32[5,2,32,128]{3,2,1,0:T(8,128)S(1)} %get-tuple-element.37), channel_id=1, source_target_pairs={{0,16},{8,24},{16,0},{24,8},{1,17},{9,25},{17,1},{25,9},{2,18},{10... | collective-permute-start | bytes 491528 | tf_op jit(solution)/shard_map/ppermute | solution.py:213
  20.9 10.8 %collective-permute-start.11 = (f32[5,2,32,128]{3,2,1,0:T(8,128)S(1)}, f32[5,2,32,128]{3,2,1,0:T(8,128)S(1)}, u32[]{:S(2)}, u32[]{:S(2)}) collective-permute-start(f32[5,2,32,128]{3,2,1,0:T(8,128)S(1)} %get-tuple-element.38), channel_id=1, source_target_pairs={{0,24},{8,0},{16,8},{24,16},{1,25},{9,1},{17,9},{25,17},{2,26},{10... | collective-permute-start | bytes 491528 | tf_op jit(solution)/shard_map/ppermute | solution.py:213
  22.3 9.4 %collective-permute-start.12 = (f32[5,2,32,128]{3,2,1,0:T(8,128)S(1)}, f32[5,2,32,128]{3,2,1,0:T(8,128)S(1)}, u32[]{:S(2)}, u32[]{:S(2)}) collective-permute-start(f32[5,2,32,128]{3,2,1,0:T(8,128)S(1)} %get-tuple-element.39), channel_id=1, source_target_pairs={{0,1},{1,2},{2,3},{3,4},{4,5},{5,6},{6,7},{8,9},{9,10},{10,11},{11... | collective-permute-start | bytes 491528 | tf_op jit(solution)/shard_map/ppermute | solution.py:232
  28.9 6.6 %collective-permute-start.13 = (f32[5,2,32,128]{3,2,1,0:T(8,128)S(1)}, f32[5,2,32,128]{3,2,1,0:T(8,128)S(1)}, u32[]{:S(2)}, u32[]{:S(2)}) collective-permute-start(f32[5,2,32,128]{3,2,1,0:T(8,128)S(1)} %get-tuple-element.40), channel_id=1, source_target_pairs={{1,0},{2,1},{3,2},{4,3},{5,4},{6,5},{7,6},{9,8},{10,9},{11,10},{12... | collective-permute-start | bytes 491528 | tf_op jit(solution)/shard_map/ppermute | solution.py:233
